TPU v7x, 32 devices: a 4x4x1 block of a 4x4x8 slice. The times are simulated.
32 devices in a mesh: part: 1 (over z), ray: 4 (over y), pix: 8 (over x, core).
Axes of the slice: x: 4, y: 4, z: 1, core: 2. Of those that a mesh axis runs over, the one named last changes fastest.
The devices are a block of a 4x4x8 slice.
Arguments:
- sys_mat: bfloat16 [23040, 9216], P('ray', 'pix')
- x_init: float32 [9216, 128], P('pix', 'part')
- sinogram: float32 [23040, 128], P('ray', 'part')
- row_inv: float32 [23040], P('ray')
- col_inv: float32 [9216], P('pix')
- relaxation: float32 [], replicated
Outputs:
- output 1: float32 [9216, 128], P('pix', 'part')
- output 2: float32 [23040, 128], P('ray', 'part')
- output 3: float32 [6, 128], P(None, 'part')
All inputs are finite; a program needn't handle non-finite values.
Results may differ from a plain program's by a relative error of at most 0.001.
Values are sent between devices in bfloat16 or wider.
A program may use at most 768 MiB of HBM per device.

v0:
```python
import jax
import jax.numpy as jnp
from jax import lax
from jax.sharding import PartitionSpec as P

SWEEPS = 6


def solution(mesh):
    ray_size = mesh.shape["ray"]

    def local_sweeps(a_blk, x_loc, sino_loc, row_inv, col_inv, relaxation):
        ray_total = a_blk.shape[0] * ray_size
        x_cur = x_loc
        sq_list = []
        residual = sino_loc
        for sweep_idx in range(SWEEPS):
            part_proj = jnp.dot(a_blk, x_cur.astype(jnp.bfloat16), preferred_element_type=jnp.float32)
            projected = lax.psum(part_proj, "pix")
            residual = row_inv[:, None] * (sino_loc - projected)
            sq_list.append(lax.psum(jnp.sum(residual * residual, axis=0), "ray") / ray_total)
            part_back = lax.dot_general(a_blk, residual.astype(jnp.bfloat16), (((0,), (0,)), ((), ())), preferred_element_type=jnp.float32)
            back_proj = lax.psum(part_back, "ray")
            x_cur = x_cur + relaxation * col_inv[:, None] * back_proj
        return x_cur, residual, jnp.stack(sq_list)

    return jax.shard_map(
        local_sweeps,
        mesh=mesh,
        in_specs=(P("ray", "pix"), P("pix", "part"), P("ray", "part"), P("ray"), P("pix"), P()),
        out_specs=(P("pix", "part"), P("ray", "part"), P(None, "part")),
        check_vma=False,
    )
```

profile of v0, /device:TPU:97, one launch (start us, length us, event | category | flops | bytes accessed | tf_op | source)
XLA Modules:
  0.0 757.0 jit_solution(13946150264409638422)
XLA Ops:
  7.2 0.1 all-reduce.14.cloned.1.call-start
  7.2 0.0 copy-start.4
  7.3 10.1 %fusion.11 = f32[5760,128]{1,0:T(8,128)} fusion(bf16[5760,1152]{1,0:T(8,128)(2,1)} %param.6, f32[1152,128]{1,0:T(8,128)} %param.7), kind=kOutput, calls=%fused_computation.40 | convolution fusion | flops 1698840576 | bytes 16809984 | tf_op jit(solution)/shard_map/dot_general | solution.py:18
  17.3 0.1 all-reduce.14.cloned.1.call-update
  17.4 0.0 copy-start.8
  17.4 0.1 all-reduce.16.cloned.1.call-start
  17.5 65.2 %all-reduce.14.cloned.1.call-done = f32[5760,128]{1,0:T(8,128)} async-done(((f32[5760,128]{1,0:T(8,128)}), f32[5760,128]{1,0:T(8,128)}) %all-reduce.14.cloned.1.call-update) | async-done | bytes 2949136 | tf_op jit(solution)/shard_map/psum | solution.py:19
  82.7 9.3 %convolution_bitcast_fusion.10 = f32[1152,128]{0,1:T(8,128)} fusion(bf16[5760,1152]{1,0:T(8,128)(2,1)} %param.6, f32[5760,128]{1,0:T(8,128)S(1)} %copy-done, f32[5760,128]{1,0:T(8,128)} %all-reduce.14.cloned.1.call-done, f32[5760]{0:T(1024)S(1)} %copy-done.4), kind=kOutput, calls=%fused_computation.22 | convolution fusion | flops 1700904960 | bytes 19782144 | tf_op jit(solution)/shard_map/dot_general | solution.py:22
  92.0 0.1 all-reduce.16.cloned.1.call-update
  92.0 0.1 all-reduce.18.cloned.1.call-start
  92.1 1.3 copy.9
  93.4 0.0 copy-start.3
  94.1 35.7 %all-reduce.16.cloned.1.call-done = f32[1152,128]{0,1:T(8,128)} async-done(((f32[1152,128]{0,1:T(8,128)}), f32[1152,128]{0,1:T(8,128)}) %all-reduce.16.cloned.1.call-update) | async-done | bytes 589840 | tf_op jit(solution)/shard_map/psum | solution.py:23
  129.8 10.2 %convolution_bitcast_fusion.4 = f32[5760,128]{1,0:T(8,128)} fusion(bf16[5760,1152]{1,0:T(8,128)(2,1)} %param.6, f32[1152,128]{0,1:T(8,128)S(1)} %copy.9, f32[1152,128]{0,1:T(8,128)} %all-reduce.16.cloned.1.call-done, f32[1152]{0:T(1024)S(1)} %broadcast_multiply_fusion), kind=kOutput, calls=%fused_computation.4 | convolution fusion | flops 1699135488 | bytes 17404416 | tf_op jit(solution)/shard_map/dot_general | solution.py:18
  140.0 0.1 all-reduce.18.cloned.1.call-update
  140.1 0.2 all-reduce.20.cloned.1.call-start
  140.3 63.7 %all-reduce.18.cloned.1.call-done = f32[5760,128]{1,0:T(8,128)} async-done(((f32[5760,128]{1,0:T(8,128)}), f32[5760,128]{1,0:T(8,128)}) %all-reduce.18.cloned.1.call-update) | async-done | bytes 2949136 | tf_op jit(solution)/shard_map/psum | solution.py:19
  204.1 9.3 %convolution_bitcast_fusion.9 = f32[1152,128]{0,1:T(8,128)} fusion(bf16[5760,1152]{1,0:T(8,128)(2,1)} %param.6, f32[5760,128]{1,0:T(8,128)S(1)} %copy-done, f32[5760,128]{1,0:T(8,128)} %all-reduce.18.cloned.1.call-done, f32[5760]{0:T(1024)S(1)} %copy-done.5), kind=kOutput, calls=%fused_computation.21 | convolution fusion | flops 1700904960 | bytes 19782144 | tf_op jit(solution)/shard_map/dot_general | solution.py:22
  213.3 0.1 all-reduce.20.cloned.1.call-update
  213.4 0.1 all-reduce.22.cloned.1.call-start
  213.5 37.7 %all-reduce.20.cloned.1.call-done = f32[1152,128]{0,1:T(8,128)} async-done(((f32[1152,128]{0,1:T(8,128)}), f32[1152,128]{0,1:T(8,128)}) %all-reduce.20.cloned.1.call-update) | async-done | bytes 589840 | tf_op jit(solution)/shard_map/psum | solution.py:23
  251.1 1.5 multiply_add_fusion.4
  252.6 10.2 %convolution_bitcast_fusion.3 = f32[5760,128]{1,0:T(8,128)} fusion(bf16[5760,1152]{1,0:T(8,128)(2,1)} %param.6, f32[1152,128]{0,1:T(8,128)S(1)} %multiply_add_fusion.4), kind=kOutput, calls=%fused_computation.3 | convolution fusion | flops 1698840576 | bytes 16809984 | tf_op jit(solution)/shard_map/dot_general | solution.py:18
  262.8 0.1 all-reduce.22.cloned.1.call-update
  262.9 0.1 all-reduce.24.cloned.1.call-start
  263.0 63.9 %all-reduce.22.cloned.1.call-done = f32[5760,128]{1,0:T(8,128)} async-done(((f32[5760,128]{1,0:T(8,128)}), f32[5760,128]{1,0:T(8,128)}) %all-reduce.22.cloned.1.call-update) | async-done | bytes 2949136 | tf_op jit(solution)/shard_map/psum | solution.py:19
  326.9 9.3 %convolution_bitcast_fusion.8 = f32[1152,128]{0,1:T(8,128)} fusion(bf16[5760,1152]{1,0:T(8,128)(2,1)} %param.6, f32[5760,128]{1,0:T(8,128)S(1)} %copy-done, f32[5760,128]{1,0:T(8,128)} %all-reduce.22.cloned.1.call-done, f32[5760]{0:T(1024)} %param.9), kind=kOutput, calls=%fused_computation.20 | convolution fusion | flops 1700904960 | bytes 19782144 | tf_op jit(solution)/shard_map/dot_general | solution.py:22
  336.2 0.1 all-reduce.24.cloned.1.call-update
  336.2 0.3 all-reduce.26.cloned.1.call-start
  336.5 37.5 %all-reduce.24.cloned.1.call-done = f32[1152,128]{0,1:T(8,128)} async-done(((f32[1152,128]{0,1:T(8,128)}), f32[1152,128]{0,1:T(8,128)}) %all-reduce.24.cloned.1.call-update) | async-done | bytes 589840 | tf_op jit(solution)/shard_map/psum | solution.py:23
  374.0 10.2 %convolution_bitcast_fusion.2 = f32[5760,128]{1,0:T(8,128)} fusion(bf16[5760,1152]{1,0:T(8,128)(2,1)} %param.6, f32[1152,128]{0,1:T(8,128)S(1)} %multiply_add_fusion.4, f32[1152,128]{0,1:T(8,128)} %all-reduce.24.cloned.1.call-done, f32[1152]{0:T(1024)S(1)} %broadcast_multiply_fusion), kind=kOutput, calls=%fused_computation.2 | convolution fusion | flops 1699135488 | bytes 17404416 | tf_op jit(solution)/shard_map/dot_general | solution.py:18
  384.2 0.1 all-reduce.26.cloned.1.call-update
  384.2 0.1 all-reduce.28.cloned.1.call-start
  384.3 63.9 %all-reduce.26.cloned.1.call-done = f32[5760,128]{1,0:T(8,128)} async-done(((f32[5760,128]{1,0:T(8,128)}), f32[5760,128]{1,0:T(8,128)}) %all-reduce.26.cloned.1.call-update) | async-done | bytes 2949136 | tf_op jit(solution)/shard_map/psum | solution.py:19
  448.2 9.3 %convolution_bitcast_fusion.7 = f32[1152,128]{0,1:T(8,128)} fusion(bf16[5760,1152]{1,0:T(8,128)(2,1)} %param.6, f32[5760,128]{1,0:T(8,128)S(1)} %copy-done, f32[5760,128]{1,0:T(8,128)} %all-reduce.26.cloned.1.call-done, f32[5760]{0:T(1024)S(1)} %copy-done.6), kind=kOutput, calls=%fused_computation.19 | convolution fusion | flops 1700904960 | bytes 19782144 | tf_op jit(solution)/shard_map/dot_general | solution.py:22
  457.5 0.1 all-reduce.28.cloned.1.call-update
  457.6 0.1 all-reduce.30.cloned.1.call-start
  457.6 37.7 %all-reduce.28.cloned.1.call-done = f32[1152,128]{0,1:T(8,128)} async-done(((f32[1152,128]{0,1:T(8,128)}), f32[1152,128]{0,1:T(8,128)}) %all-reduce.28.cloned.1.call-update) | async-done | bytes 589840 | tf_op jit(solution)/shard_map/psum | solution.py:23
  495.3 1.5 multiply_add_fusion.2
  496.8 10.0 %convolution_bitcast_fusion.1 = f32[5760,128]{1,0:T(8,128)} fusion(bf16[5760,1152]{1,0:T(8,128)(2,1)} %param.6, f32[1152,128]{0,1:T(8,128)S(1)} %multiply_add_fusion.2), kind=kOutput, calls=%fused_computation.1 | convolution fusion | flops 1698840576 | bytes 16809984 | tf_op jit(solution)/shard_map/dot_general | solution.py:18
  506.8 0.1 all-reduce.30.cloned.1.call-update
  506.9 0.3 all-reduce.32.cloned.1.call-start
  507.2 63.7 %all-reduce.30.cloned.1.call-done = f32[5760,128]{1,0:T(8,128)} async-done(((f32[5760,128]{1,0:T(8,128)}), f32[5760,128]{1,0:T(8,128)}) %all-reduce.30.cloned.1.call-update) | async-done | bytes 2949136 | tf_op jit(solution)/shard_map/psum | solution.py:19
  570.9 9.3 %convolution_bitcast_fusion.6 = f32[1152,128]{0,1:T(8,128)} fusion(bf16[5760,1152]{1,0:T(8,128)(2,1)} %param.6, f32[5760,128]{1,0:T(8,128)S(1)} %copy-done, f32[5760,128]{1,0:T(8,128)} %all-reduce.30.cloned.1.call-done, f32[5760]{0:T(1024)} %param.9), kind=kOutput, calls=%fused_computation.18 | convolution fusion | flops 1700904960 | bytes 19782144 | tf_op jit(solution)/shard_map/dot_general | solution.py:22
  580.2 0.1 all-reduce.32.cloned.1.call-update
  580.2 0.1 all-reduce.34.cloned.1.call-start
  580.3 37.7 %all-reduce.32.cloned.1.call-done = f32[1152,128]{0,1:T(8,128)} async-done(((f32[1152,128]{0,1:T(8,128)}), f32[1152,128]{0,1:T(8,128)}) %all-reduce.32.cloned.1.call-update) | async-done | bytes 589840 | tf_op jit(solution)/shard_map/psum | solution.py:23
  618.0 10.2 %convolution_bitcast_fusion = f32[5760,128]{1,0:T(8,128)} fusion(bf16[5760,1152]{1,0:T(8,128)(2,1)} %param.6, f32[1152,128]{0,1:T(8,128)S(1)} %multiply_add_fusion.2, f32[1152,128]{0,1:T(8,128)} %all-reduce.32.cloned.1.call-done, f32[1152]{0:T(1024)S(1)} %broadcast_multiply_fusion), kind=kOutput, calls=%fused_computation | convolution fusion | flops 1699135488 | bytes 17404416 | tf_op jit(solution)/shard_map/dot_general | solution.py:18
  628.2 0.1 all-reduce.34.cloned.1.call-update
  628.2 0.1 all-reduce.36.cloned.1.call-start
  628.3 63.9 %all-reduce.34.cloned.1.call-done = f32[5760,128]{1,0:T(8,128)} async-done(((f32[5760,128]{1,0:T(8,128)}), f32[5760,128]{1,0:T(8,128)}) %all-reduce.34.cloned.1.call-update) | async-done | bytes 2949136 | tf_op jit(solution)/shard_map/psum | solution.py:19
  692.2 8.0 %multiply_reduce_fusion.1 = (f32[128]{0:T(128)S(1)}, f32[128]{0:T(128)S(1)}, f32[128]{0:T(128)}, f32[128]{0:T(128)}, f32[128]{0:T(128)}, /*index=5*/f32[128]{0:T(128)}, f32[5760,128]{1,0:T(8,128)S(1)}) fusion(f32[5760,128]{1,0:T(8,128)S(1)} %copy-done, f32[5760,128]{1,0:T(8,128)} %all-reduce.30.cloned.1.call-done, f32[5760]{0:T(1024)} %param.9, ...), kind=kLoop, calls=%fused_computation.6 | loop fusion | flops 17693952 | bytes 23619072 | tf_op jit(solution)/shard_map/reduce_sum | solution.py:21
  700.3 1.6 copy-done.1
  701.9 7.9 %convolution_bitcast_fusion.5 = f32[1152,128]{0,1:T(8,128)} fusion(bf16[5760,1152]{1,0:T(8,128)(2,1)} %param.6, f32[5760,128]{1,0:T(8,128)S(1)} %get-tuple-element.20), kind=kOutput, calls=%fused_computation.17 | convolution fusion | flops 1699430400 | bytes 16809984 | tf_op jit(solution)/shard_map/dot_general | solution.py:22
  709.7 0.1 all-reduce.36.cloned.1.call-update
  709.8 0.0 copy-done.9
  709.8 0.0 copy-done.10
  709.8 0.0 copy-done.11
  709.8 0.0 copy-done.12
  709.8 8.8 %all-reduce = (f32[128]{0:T(128)S(1)}, f32[128]{0:T(128)S(1)}, f32[128]{0:T(128)S(1)}, f32[128]{0:T(128)S(1)}, f32[128]{0:T(128)S(1)}, /*index=5*/f32[128]{0:T(128)S(1)}) all-reduce(f32[128]{0:T(128)S(1)} %copy-done.11, f32[128]{0:T(128)S(1)} %copy-done.10, f32[128]{0:T(128)S(1)} %copy-done.9, ...), channel_id=1, replica_groups=mesh['part'=1,'ray'=4,'pix'=8] {'ray'}, use_global_device_ids=true, to_apply=%region_13.0 | all-reduce | flops 768 | bytes 6144 | tf_op jit(solution)/shard_map/psum | solution.py:21
  718.7 0.6 stack.27
  719.3 28.2 %all-reduce.36.cloned.1.call-done = f32[1152,128]{0,1:T(8,128)} async-done(((f32[1152,128]{0,1:T(8,128)}), f32[1152,128]{0,1:T(8,128)}) %all-reduce.36.cloned.1.call-update) | async-done | bytes 589840 | tf_op jit(solution)/shard_map/psum | solution.py:23
  747.5 1.1 multiply_add_fusion
  748.7 1.1 copy.15
  (22 shorter events, 0.1 us)
Async XLA Ops:
  7.2 75.5 %all-reduce.14.cloned.1.call-start = ((), (), s32[]{:S(2)}) async-start(), calls=%async_computation | async-start | bytes 5898240 | tf_op jit(solution)/shard_map/psum | solution.py:19
  7.2 75.4 %copy-start.4 = (f32[5760]{0:T(1024)S(1)}, f32[5760]{0:T(1024)}, u32[]{:S(2)}) copy-start(f32[5760]{0:T(1024)} %param.9) | copy-start | bytes 69124
  17.3 65.4 %copy-start = (f32[5760,128]{1,0:T(8,128)S(1)}, f32[5760,128]{1,0:T(8,128)}, u32[]{:S(2)}) copy-start(f32[5760,128]{1,0:T(8,128)} %param.8) | copy-start | bytes 8847364
  17.4 76.7 %copy-start.8 = (f32[1152]{0:T(1024)S(1)}, f32[1152]{0:T(1024)}, u32[]{:S(2)}) copy-start(f32[1152]{0:T(1024)} %param.10) | copy-start | bytes 13828
  17.4 112.4 %all-reduce.16.cloned.1.call-start = ((), (), s32[]{:S(2)}) async-start(), calls=%async_computation.1 | async-start | bytes 1179648 | tf_op jit(solution)/shard_map/psum | solution.py:23
  92.0 112.0 %all-reduce.18.cloned.1.call-start = ((), (), s32[]{:S(2)}) async-start(), calls=%async_computation.2 | async-start | bytes 5898240 | tf_op jit(solution)/shard_map/psum | solution.py:19
  93.4 46.6 %copy-start.3 = (f32[1152,128]{0,1:T(8,128)}, f32[1152,128]{0,1:T(8,128)S(1)}, u32[]{:S(2)}) copy-start(f32[1152,128]{0,1:T(8,128)S(1)} %copy.9) | copy-start | bytes 1769476
  140.0 64.1 %copy-start.5 = (f32[5760]{0:T(1024)S(1)}, f32[5760]{0:T(1024)}, u32[]{:S(2)}) copy-start(f32[5760]{0:T(1024)} %param.9) | copy-start | bytes 69124
  140.1 111.1 %all-reduce.20.cloned.1.call-start = ((), (), s32[]{:S(2)}) async-start(), calls=%async_computation.3 | async-start | bytes 1179648 | tf_op jit(solution)/shard_map/psum | solution.py:23
  213.4 113.5 %all-reduce.22.cloned.1.call-start = ((), (), s32[]{:S(2)}) async-start(), calls=%async_computation.4 | async-start | bytes 5898240 | tf_op jit(solution)/shard_map/psum | solution.py:19
  252.6 121.4 %copy-start.2 = (f32[1152,128]{0,1:T(8,128)}, f32[1152,128]{0,1:T(8,128)S(1)}, u32[]{:S(2)}) copy-start(f32[1152,128]{0,1:T(8,128)S(1)} %multiply_add_fusion.4) | copy-start | bytes 1769476
  262.9 111.1 %all-reduce.24.cloned.1.call-start = ((), (), s32[]{:S(2)}) async-start(), calls=%async_computation.5 | async-start | bytes 1179648 | tf_op jit(solution)/shard_map/psum | solution.py:23
  336.2 112.0 %all-reduce.26.cloned.1.call-start = ((), (), s32[]{:S(2)}) async-start(), calls=%async_computation.6 | async-start | bytes 5898240 | tf_op jit(solution)/shard_map/psum | solution.py:19
  384.2 64.1 %copy-start.6 = (f32[5760]{0:T(1024)S(1)}, f32[5760]{0:T(1024)}, u32[]{:S(2)}) copy-start(f32[5760]{0:T(1024)} %param.9) | copy-start | bytes 69124
  384.2 111.1 %all-reduce.28.cloned.1.call-start = ((), (), s32[]{:S(2)}) async-start(), calls=%async_computation.7 | async-start | bytes 1179648 | tf_op jit(solution)/shard_map/psum | solution.py:23
  457.6 113.3 %all-reduce.30.cloned.1.call-start = ((), (), s32[]{:S(2)}) async-start(), calls=%async_computation.8 | async-start | bytes 5898240 | tf_op jit(solution)/shard_map/psum | solution.py:19
  506.9 111.1 %all-reduce.32.cloned.1.call-start = ((), (), s32[]{:S(2)}) async-start(), calls=%async_computation.9 | async-start | bytes 1179648 | tf_op jit(solution)/shard_map/psum | solution.py:23
  580.2 112.0 %all-reduce.34.cloned.1.call-start = ((), (), s32[]{:S(2)}) async-start(), calls=%async_computation.10 | async-start | bytes 5898240 | tf_op jit(solution)/shard_map/psum | solution.py:19
  628.2 119.3 %all-reduce.36.cloned.1.call-start = ((), (), s32[]{:S(2)}) async-start(), calls=%async_computation.11 | async-start | bytes 1179648 | tf_op jit(solution)/shard_map/psum | solution.py:23
  700.3 1.6 copy-start.1
  701.9 8.0 %copy-start.9 = (f32[128]{0:T(128)S(1)}, f32[128]{0:T(128)}, u32[]{:S(2)}) copy-start(f32[128]{0:T(128)} %get-tuple-element.8) | copy-start | bytes 1540
  701.9 8.0 %copy-start.10 = (f32[128]{0:T(128)S(1)}, f32[128]{0:T(128)}, u32[]{:S(2)}) copy-start(f32[128]{0:T(128)} %get-tuple-element.9) | copy-start | bytes 1540
  701.9 8.0 %copy-start.11 = (f32[128]{0:T(128)S(1)}, f32[128]{0:T(128)}, u32[]{:S(2)}) copy-start(f32[128]{0:T(128)} %get-tuple-element.10) | copy-start | bytes 1540
  701.9 8.0 %copy-start.12 = (f32[128]{0:T(128)S(1)}, f32[128]{0:T(128)}, u32[]{:S(2)}) copy-start(f32[128]{0:T(128)} %get-tuple-element.19) | copy-start | bytes 1540
  701.9 45.7 %copy-start.7 = (f32[1152,128]{0,1:T(8,128)S(1)}, f32[1152,128]{0,1:T(8,128)}, u32[]{:S(2)}) copy-start(f32[1152,128]{0,1:T(8,128)} %all-reduce.32.cloned.1.call-done) | copy-start | bytes 1769476
Sparse Core Ops, SparseCore 0:
  17.5 65.1 all-reduce.13
  92.1 37.5 all-reduce.15
  140.2 63.8 all-reduce.17
  213.5 37.5 all-reduce.19
  263.0 63.8 all-reduce.21
  336.4 37.5 all-reduce.23
  384.4 63.8 all-reduce.25
  457.7 37.5 all-reduce.27
  507.0 63.8 all-reduce.29
  580.3 37.5 all-reduce.31
  628.4 63.8 all-reduce.33
  709.9 37.5 all-reduce.35
where the time goes:
time: 766 us; the launch traced here: 757 us
  waiting for transfers between devices  599 us (78%)
  matrix products  115 us (15%)
  between operations  15.4 us (2%)
  other arithmetic  12.2 us (2%)
  blocking collectives  8.83 us (1%)
    psum x6, waiting for transfers between devices, local_sweeps(): projected = lax.psum(part_proj, 'pix')  384 us
    psum x6, waiting for transfers between devices, local_sweeps(): back_proj = lax.psum(part_back, 'ray')  214 us
    dot_general x6, matrix products, local_sweeps(): jnp.dot(a_blk, x_cur.astype(jnp.bfloat16), preferred_element_type=jnp.flo...  60.9 us
    dot_general x6, matrix products, local_sweeps(): lax.dot_general(a_blk, residual.astype(jnp.bfloat16), (((0,), (0,)), ((),...  54.3 us
  transfers between devices with their start and end apart: 12, of which 12 were waited for; matrix products, arithmetic and copies ran while one was open for 0% of the time, Pallas kernels for 0%

commit v1 on v0

v1 whole, which is shorter than its diff:
```python
import functools

import jax
import jax.numpy as jnp
from jax import lax
from jax.experimental import pallas as pl
from jax.experimental.pallas import tpu as pltpu
from jax.sharding import PartitionSpec as P

SWEEPS = 6
MESH = pl.DeviceIdType.MESH
F32 = jnp.float32
BF16 = jnp.bfloat16

CHUNKS = ((0, 240, 128), (240, 240, 112), (480, 240, 128))


class Lazy:
    def __init__(self, makers):
        self.makers = makers

    def __getitem__(self, key):
        return self.makers[key]()

    def values(self):
        return [make() for make in self.makers.values()]


def _kernel(ring_x, ring_y, ray_total, a_hbm, x_in, b_hbm, rinv, cinv, lam, x_out, r_out, s_out,
            a_v, b_v, ps, pd, ss, q, fl, fr, rall, rf, gt, qy, fyl, fyr, xs, xb, xf, xn, sqv, sqr, sqc,
            a_sem, b_sem, o_sem, send, recv):
    rp = ss.shape[1]
    cy = gt.shape[1]
    width = gt.shape[2]
    n_x, n_y = ring_x // 2, ring_y
    pix = lax.axis_index("pix")
    y = lax.axis_index("ray")
    x, c = pix // 2, lax.rem(pix, 2)
    xr, xl, xo = lax.rem(x + 1, n_x), lax.rem(x + n_x - 1, n_x), lax.rem(x + 2, n_x)
    yr, yl, yo = lax.rem(y + 1, n_y), lax.rem(y + n_y - 1, n_y), lax.rem(y + 2, n_y)
    right, left, sib = {"pix": xr * 2 + c}, {"pix": xl * 2 + c}, {"pix": x * 2 + 1 - c}
    up, down = {"ray": yr}, {"ray": yl}
    mine, theirs = c * n_x, (1 - c) * n_x
    k_chunks = range(len(CHUNKS))

    names = {}

    def tx(name, k, src, dst, dev):
        slot = names.setdefault((name, k), len(names))
        return pltpu.make_async_remote_copy(
            src_ref=src, dst_ref=dst, send_sem=send.at[slot], recv_sem=recv.at[slot],
            device_id=dev, device_id_type=MESH)

    def rows(k):
        o, n, _ = CHUNKS[k]
        return pl.ds(o, n)

    def h0(k):
        o, _, n0 = CHUNKS[k]
        return pl.ds(o, n0)

    def h1(k):
        o, n, n0 = CHUNKS[k]
        return pl.ds(o + n0, n - n0)

    def t_p(k, d):
        return tx("p", (k, d), ps.at[d, rows(k)], pd.at[d, rows(k)], sib)

    def t_x1r(k):
        return tx("x1r", k, ss.at[xo, h1(k)], q.at[h1(k)], right)

    def t_x1l(k):
        return tx("x1l", k, ss.at[xo, h0(k)], q.at[h0(k)], left)

    def t_xdr(k):
        return tx("xdr", k, ss.at[xr, h0(k)], fl.at[h0(k)], right)

    def t_xdl(k):
        return tx("xdl", k, ss.at[xl, h1(k)], fr.at[h1(k)], left)

    def t_x2r(k):
        return tx("x2r", k, ss.at[xr, h1(k)], fl.at[h1(k)], right)

    def t_x2l(k):
        return tx("x2l", k, ss.at[xl, h0(k)], fr.at[h0(k)], left)

    def gather(name, k, buf, sel, dev):
        return tx(name, k, buf.at[sel], buf.at[sel], dev)

    def t_g(k, buf=None, tag="g"):
        buf = rall if buf is None else buf
        return Lazy({
            "r": lambda: gather(tag + "r", k, buf, (mine + x, rows(k)), right),
            "l": lambda: gather(tag + "l", k, buf, (mine + x, rows(k)), left),
            "s": lambda: gather(tag + "s", k, buf, (mine + x, rows(k)), sib),
            "hr": lambda: gather(tag + "hr", k, buf, (mine + xl, h1(k)), right),
            "hl": lambda: gather(tag + "hl", k, buf, (mine + xr, h0(k)), left),
            "sl": lambda: gather(tag + "sl", k, buf, (mine + xl, rows(k)), sib),
            "sr": lambda: gather(tag + "sr", k, buf, (mine + xr, rows(k)), sib),
            "so": lambda: gather(tag + "so", k, buf, (mine + xo, rows(k)), sib),
        })

    half = cy // 2
    yh0, yh1 = pl.ds(0, half), pl.ds(half, cy - half)
    lane0 = (width // 256 + (1 if width % 256 else 0)) * 128
    lane_a, lane_b = pl.ds(0, lane0), pl.ds(lane0, width - lane0)

    t_y1r = lambda: tx("y1r", 0, gt.at[yo, yh1], qy.at[yh1], up)
    t_y1l = lambda: tx("y1l", 0, gt.at[yo, yh0], qy.at[yh0], down)
    t_ydr = lambda: tx("ydr", 0, gt.at[yr, yh0], fyl.at[yh0], up)
    t_ydl = lambda: tx("ydl", 0, gt.at[yl, yh1], fyr.at[yh1], down)
    t_y2r = lambda: tx("y2r", 0, gt.at[yr, yh1], fyl.at[yh1], up)
    t_y2l = lambda: tx("y2l", 0, gt.at[yl, yh0], fyr.at[yh0], down)

    def t_z(buf, tag):
        every = pl.ds(0, cy)
        return Lazy({
            "r": lambda: gather(tag + "r", 0, buf, (y,), up),
            "l": lambda: gather(tag + "l", 0, buf, (y,), down),
            "hr": lambda: gather(tag + "hr", 0, buf, (yl, every, lane_b), up),
            "hl": lambda: gather(tag + "hl", 0, buf, (yr, every, lane_a), down),
        })

    barrier = pltpu.get_barrier_semaphore()
    for j in range(1, ring_x):
        pl.semaphore_signal(barrier, inc=1, device_id={"pix": lax.rem(pix + j, ring_x)}, device_id_type=MESH)
    for j in range(1, ring_y):
        pl.semaphore_signal(barrier, inc=1, device_id={"ray": lax.rem(y + j, ring_y)}, device_id_type=MESH)

    def load_a(o, k):
        return pltpu.make_async_copy(a_hbm.at[o, rows(k)], a_v.at[o, rows(k)], a_sem.at[k, o])

    def start_a(k, base):
        def one(d, _):
            load_a(base + d, k).start()
            return 0
        lax.fori_loop(0, n_x, one, 0)

    for k in k_chunks:
        start_a(k, theirs)
        start_a(k, mine)
    load_b = pltpu.make_async_copy(b_hbm.at[mine + x], b_v, b_sem)
    load_b.start()

    xn[...] = x_in[...].astype(BF16)
    xf[...] = x_in[...].T.reshape(xf.shape)
    xs[...] = xf[y]
    sqv[...] = jnp.zeros_like(sqv)
    load_b.wait()
    pl.semaphore_wait(barrier, ring_x - 1 + ring_y - 1)

    def project(s, k, base, dst, first):
        def one(d, _):
            if first:
                load_a(base + d, k).wait()
            dst[d, rows(k)] = jnp.dot(a_v[base + d, rows(k)], xn[...], preferred_element_type=F32)
            return 0
        lax.fori_loop(0, n_x, one, 0)

    def sweep(s, first, last):
        def F_sib(k):
            project(s, k, theirs, ps, first)
            for d in range(n_x):
                t_p(k, d).start()

        def F_own(k):
            project(s, k, mine, ss, first)

        def D(k):
            for d in range(n_x):
                t_p(k, d).wait_recv()
            for d in range(n_x):
                ss[d, rows(k)] = ss[d, rows(k)] + pd[d, rows(k)]
            t_x1r(k).start()
            t_x1l(k).start()
            t_xdr(k).start()
            t_xdl(k).start()

        def L(k):
            t_x1r(k).wait_recv()
            ss[xr, h1(k)] = ss[xr, h1(k)] + q[h1(k)]
            t_x2r(k).start()
            t_x1l(k).wait_recv()
            ss[xl, h0(k)] = ss[xl, h0(k)] + q[h0(k)]
            t_x2l(k).start()

        def O(k):
            t_xdr(k).wait_recv()
            t_xdl(k).wait_recv()
            t_x2r(k).wait_recv()
            t_x2l(k).wait_recv()
            total = ss[x, rows(k)] + fl[rows(k)] + fr[rows(k)]
            r = rinv[rows(k)] * (b_v[rows(k)] - total)
            rall[mine + x, rows(k)] = r.astype(BF16)
            part = jnp.sum(r * r, axis=0, keepdims=True)
            if k == 0:
                sqv[pl.ds(s, 1)] = part
            else:
                sqv[pl.ds(s, 1)] = sqv[pl.ds(s, 1)] + part
            if last:
                rf[mine + x, rows(k)] = r
            t = t_g(k)
            t["r"].start()
            t["l"].start()
            t["s"].start()

        def A(k, buf=None, tag="g"):
            t = t_g(k, buf, tag)
            t["r"].wait_recv()
            t["hr"].start()
            t["sl"].start()
            t["l"].wait_recv()
            t["hl"].start()
            t["sr"].start()

        def A2(k, buf=None, tag="g"):
            t = t_g(k, buf, tag)
            t["hr"].wait_recv()
            t["hl"].wait_recv()
            t["so"].start()

        def back(o, k, init=False):
            part = lax.dot_general(rall[o, rows(k)], a_v[o, rows(k)], (((0,), (0,)), ((), ())),
                                   preferred_element_type=F32).reshape(gt.shape)
            if init:
                gt[...] = part
            else:
                gt[...] = gt[...] + part

        def B_own(k):
            back(mine + x, k, init=(k == 0))

        def B_near(k):
            back(mine + xl, k)
            back(mine + xr, k)

        def B_far(k):
            t = t_g(k)
            t["s"].wait_recv()
            back(theirs + x, k)
            t["sl"].wait_recv()
            back(theirs + xl, k)
            t["sr"].wait_recv()
            back(theirs + xr, k)
            back(mine + xo, k)
            t["so"].wait_recv()
            back(theirs + xo, k)

        F_sib(0); F_own(0); F_sib(1); D(0); F_own(1); F_sib(2); D(1); L(0); F_own(2); D(2); L(1)
        O(0); B_own(0); L(2); A(0); O(1); B_near(0); A2(0); A(1); O(2); B_far(0)
        B_own(1); B_near(1); A2(1); A(2); B_own(2); B_far(1); A2(2); B_near(2); B_far(2)

        t_y1r().start()
        t_y1l().start()
        t_ydr().start()
        t_ydl().start()
        if last:
            for k in k_chunks:
                t = t_g(k, rf, "f")
                t["r"].start()
                t["l"].start()
                t["s"].start()
        t_y1r().wait_recv()
        gt[yr, yh1] = gt[yr, yh1] + qy[yh1]
        t_y2r().start()
        t_y1l().wait_recv()
        gt[yl, yh0] = gt[yl, yh0] + qy[yh0]
        t_y2l().start()
        t_ydr().wait_recv()
        t_ydl().wait_recv()
        t_y2r().wait_recv()
        t_y2l().wait_recv()
        xs[...] = xs[...] + lam[0] * cinv[...] * (gt[y] + fyl[...] + fyr[...])
        if last:
            buf, tag = xf, "w"
            xf[y] = xs[...]
        else:
            buf, tag = xb, "z"
            xb[y] = xs[...].astype(BF16)
        z = t_z(buf, tag)
        z["r"].start()
        z["l"].start()
        if last:
            sq_sends = squares()
            for k in k_chunks:
                A(k, rf, "f")
        z["r"].wait_recv()
        z["hr"].start()
        z["l"].wait_recv()
        z["hl"].start()
        if last:
            for k in k_chunks:
                A2(k, rf, "f")
        z["hr"].wait_recv()
        z["hl"].wait_recv()
        if last:
            x_out[...] = xf[...].reshape(cy * n_y, width).T
            for k in k_chunks:
                t = t_g(k, rf, "f")
                for key in ("s", "sl", "sr", "so"):
                    t[key].wait_recv()
            out = pltpu.make_async_copy(rf, r_out, o_sem)
            out.start()
            out.wait()
        else:
            xn[...] = xb[...].reshape(cy * n_y, width).T

        for k in k_chunks:
            for d in range(n_x):
                t_p(k, d).wait_send()
            for t in (t_x1r, t_x1l, t_xdr, t_xdl, t_x2r, t_x2l):
                t(k).wait_send()
            for t in t_g(k).values():
                t.wait_send()
            if last:
                for t in t_g(k, rf, "f").values():
                    t.wait_send()
        for t in (t_y1r, t_y1l, t_ydr, t_ydl, t_y2r, t_y2l):
            t().wait_send()
        for t in z.values():
            t.wait_send()
        if last:
            for t in sq_sends:
                t.wait_send()

    def squares():
        sends = []
        sqr[pix] = sqv[...]
        for j in range(1, ring_x):
            t = tx("qx", j, sqr.at[pix], sqr.at[pix], {"pix": lax.rem(pix + j, ring_x)})
            t.start()
            sends.append(t)
        for t in sends:
            t.wait_recv()
        total = sqr[0]
        for j in range(1, ring_x):
            total = total + sqr[j]
        sqc[y] = total
        more = []
        for j in range(1, ring_y):
            t = tx("qy", j, sqc.at[y], sqc.at[y], {"ray": lax.rem(y + j, ring_y)})
            t.start()
            more.append(t)
        for t in more:
            t.wait_recv()
        total = sqc[0]
        for j in range(1, ring_y):
            total = total + sqc[j]
        s_out[...] = (total / ray_total)[:SWEEPS]
        return sends + more

    sweep(0, True, False)

    def body(s, _):
        sweep(s, False, False)
        return 0

    lax.fori_loop(1, SWEEPS - 1, body, 0)
    sweep(SWEEPS - 1, False, True)


def solution(mesh):
    ring_x, ring_y = mesh.shape["pix"], mesh.shape["ray"]

    def local_sweeps(a_blk, x_loc, sino_loc, row_inv, col_inv, relaxation):
        rays, width = a_blk.shape
        cols = x_loc.shape[1]
        rp, cy, n_x = rays // ring_x, cols // ring_y, ring_x // 2
        pix = lax.axis_index("pix")
        owner = lax.rem(pix, 2) * n_x + pix // 2
        rinv = jnp.broadcast_to(lax.dynamic_slice(row_inv, (owner * rp,), (rp,))[:, None], (rp, cols))
        cinv = jnp.broadcast_to(col_inv[None, :], (cy, width))
        vmem = pl.BlockSpec(memory_space=pltpu.VMEM)
        hbm = pl.BlockSpec(memory_space=pl.ANY)
        smem = pl.BlockSpec(memory_space=pltpu.SMEM)
        x_fin, resid, sq = pl.pallas_call(
            functools.partial(_kernel, ring_x, ring_y, rays * ring_y),
            out_shape=(
                jax.ShapeDtypeStruct((width, cols), F32),
                jax.ShapeDtypeStruct((ring_x, rp, cols), F32),
                jax.ShapeDtypeStruct((SWEEPS, cols), F32),
            ),
            in_specs=[hbm, vmem, hbm, vmem, vmem, smem],
            out_specs=(vmem, hbm, vmem),
            scratch_shapes=[
                pltpu.VMEM((ring_x, rp, width), BF16),
                pltpu.VMEM((rp, cols), F32),
                pltpu.VMEM((n_x, rp, cols), F32),
                pltpu.VMEM((n_x, rp, cols), F32),
                pltpu.VMEM((n_x, rp, cols), F32),
                pltpu.VMEM((rp, cols), F32),
                pltpu.VMEM((rp, cols), F32),
                pltpu.VMEM((rp, cols), F32),
                pltpu.VMEM((ring_x, rp, cols), BF16),
                pltpu.VMEM((ring_x, rp, cols), F32),
                pltpu.VMEM((ring_y, cy, width), F32),
                pltpu.VMEM((cy, width), F32),
                pltpu.VMEM((cy, width), F32),
                pltpu.VMEM((cy, width), F32),
                pltpu.VMEM((cy, width), F32),
                pltpu.VMEM((ring_y, cy, width), BF16),
                pltpu.VMEM((ring_y, cy, width), F32),
                pltpu.VMEM((width, cols), BF16),
                pltpu.VMEM((8, cols), F32),
                pltpu.VMEM((ring_x, 8, cols), F32),
                pltpu.VMEM((ring_y, 8, cols), F32),
                pltpu.SemaphoreType.DMA((len(CHUNKS), ring_x)),
                pltpu.SemaphoreType.DMA,
                pltpu.SemaphoreType.DMA,
                pltpu.SemaphoreType.DMA((128,)),
                pltpu.SemaphoreType.DMA((128,)),
            ],
            compiler_params=pltpu.CompilerParams(
                collective_id=0, has_side_effects=True, vmem_limit_bytes=60 * 1024 * 1024),
        )(a_blk.reshape(ring_x, rp, width), x_loc, sino_loc.reshape(ring_x, rp, cols), rinv, cinv, relaxation.reshape(1))
        return x_fin, resid.reshape(rays, cols), sq

    return jax.shard_map(
        local_sweeps,
        mesh=mesh,
        in_specs=(P("ray", "pix"), P("pix", "part"), P("ray", "part"), P("ray"), P("pix"), P()),
        out_specs=(P("pix", "part"), P("ray", "part"), P(None, "part")),
        check_vma=False,
    )
```

time: 766 us -> 329 us (0.43); the launches traced: 757 us -> 328 us
  waiting for transfers between devices: 599 us -> 0 us
  Pallas kernels: 0 us -> 318 us
  matrix products: 115 us -> 0 us
  between operations: 15.4 us -> 1.31 us
  other arithmetic: 12.2 us -> 0 us
  blocking collectives: 8.83 us -> 0 us
    psum x12 -> x0, waiting for transfers between devices: 599 us -> none  [the longest x6 384 us: local_sweeps(): projected = lax.psum(part_proj, 'pix')]
    pallas_call x0 -> x1, Pallas kernels: none -> 318 us  [local_sweeps(): pl.pallas_call(functools.partial(_kernel, ring_x, ring_y, rays * ring_y),...]
    dot_general x12 -> x0, matrix products: 115 us -> none  [the longest x6 60.9 us: local_sweeps(): jnp.dot(a_blk, x_cur.astype(jnp.bfloat16), preferred_element_type=jnp.flo...]
    psum x1 -> x0, blocking collectives: 8.83 us -> none  [local_sweeps(): lax.psum(jnp.sum(residual * residual, axis=0), 'ray') / ray_total]
    reduce_sum x1 -> x0, other arithmetic: 8.03 us -> none  [local_sweeps(): jnp.sum(residual * residual, axis=0)]
  transfers between devices with their start and end apart: 12 -> 0, of which waited for: 12 -> 0; matrix products, arithmetic and copies ran while one was open for 0% -> 0% of each run, Pallas kernels for 0% -> 0%
where the time goes in v1:
time: 329 us; the launch traced here: 328 us
  Pallas kernels  318 us (97%)
  local copies, waits for them, and re-layouts  9.18 us (3%)
    pallas_call x1, Pallas kernels, local_sweeps(): pl.pallas_call(functools.partial(_kernel, ring_x, ring_y, rays * ring_y),...  318 us

profile of v1, /device:TPU:97, one launch (start us, length us, event | category | flops | bytes accessed | tf_op | source)
XLA Modules:
  0.0 328.5 jit_solution(10175785165929348881)
XLA Ops:
  1.3 0.8 dynamic_slice.3
  2.1 1.4 broadcast_in_dim.5.cinv
  3.4 0.9 broadcast_in_dim.4.rinv
  4.3 318.0 %shard_map.85 = (f32[1152,128]{1,0:T(8,128)}, f32[8,720,128]{2,1,0:T(8,128)}, f32[6,128]{1,0:T(8,128)}) custom-call(bf16[8,720,1152]{2,1,0:T(8,128)(2,1)} %bitcast.5, f32[1152,128]{1,0:T(8,128)} %x_in.1, f32[8,720,128]{2,1,0:T(8,128)} %bitcast.6, f32[720,128]{1,0:T(8,128)} %broadcast_in_dim.4.rinv, f32[32,1152]{1,0:T(8,128)} %broadcast_in_dim.5.cinv, ...), custom_call_target="tpu_custom_call" | custom-call | tf_op jit(solution)/shard_map/pallas_call | solution.py:376
  322.3 1.9 copy.13
  324.2 0.0 copy-start
  324.2 3.6 %copy.14 = f32[5760,128]{1,0:T(8,128)} copy(f32[5760,128]{1,0:T(8,128)} %bitcast.7) | data formatting | bytes 5898240
  327.9 0.0 copy-done
  327.9 0.6 copy.15
Async XLA Ops:
  324.2 3.6 %copy-start = (f32[6,128]{1,0:T(8,128)S(1)}, f32[6,128]{1,0:T(8,128)}, u32[]{:S(2)}) copy-start(f32[6,128]{1,0:T(8,128)} %get-tuple-element.14) | copy-start | bytes 9220

commit v2 on v0

v2 whole, which is shorter than its diff:
```python
import functools

import jax
import jax.numpy as jnp
from jax import lax
from jax.experimental import pallas as pl
from jax.experimental.pallas import tpu as pltpu
from jax.sharding import PartitionSpec as P

SWEEPS = 6
GROUPS = 2
MESH = pl.DeviceIdType.MESH
F32 = jnp.float32
BF16 = jnp.bfloat16

CHUNKS = ((0, 128), (128, 128), (256, 112))


def _kernel(ring_x, ring_y, ray_total, a_hbm, x_in, b_hbm, rinv_in, cinv, lam, x_out, r_out, s_out,
            a_v, b_v, rinv, bp, ps, pd, ss, fin, rall, rf, gt, fy, xs, xb, xf, xn, sqv, sqr, sqc,
            a_sem, b_sem, x_sem, r_sem, send, recv):
    own_rows = b_hbm.shape[1]
    packed = ss.shape[2]
    lanes = ss.shape[3]
    half = lanes // GROUPS
    cy, width = gt.shape[2], gt.shape[3]
    n_x, n_y = ring_x // 2, ring_y
    pix = lax.axis_index("pix")
    y = lax.axis_index("ray")
    x, c = pix // 2, lax.rem(pix, 2)
    sib = {"pix": x * 2 + 1 - c}
    mine, theirs = c * n_x, (1 - c) * n_x
    chunks = range(len(CHUNKS))
    others_x, others_y = range(1, n_x), range(1, n_y)

    def at_x(j):
        return lax.rem(x + j, n_x)

    def at_y(j):
        return lax.rem(y + j, n_y)

    def core_at(j):
        return {"pix": at_x(j) * 2 + c}

    names = {}

    def tx(name, src, dst, dev):
        slot = names.setdefault(name, len(names))
        return pltpu.make_async_remote_copy(
            src_ref=src, dst_ref=dst, send_sem=send.at[slot], recv_sem=recv.at[slot],
            device_id=dev, device_id_type=MESH)

    def rows(k):
        return pl.ds(*CHUNKS[k])

    def low_rows(k):
        return pl.ds(packed + CHUNKS[k][0], CHUNKS[k][1])

    def t_p(g, k):
        return tx(("p", g, k), ps.at[g, :, rows(k)], pd.at[g, :, rows(k)], sib)

    def t_x(g, k, j):
        return tx(("x", g, k, j), ss.at[g, at_x(j), rows(k)], fin.at[g, j - 1, rows(k)], core_at(j))

    def t_r(g, k, j):
        ref = rall.at[g, mine + x, rows(k)]
        return tx(("r", g, k, j), ref, ref, core_at(j))

    def t_s(g, k, j):
        ref = rall.at[g, mine + at_x(n_x - j), rows(k)]
        return tx(("s", g, k, j), ref, ref, sib)

    def t_rf(g, j):
        ref = rf.at[g, mine + x]
        return tx(("rf", g, j), ref, ref, core_at(j))

    def t_sf(g, j):
        ref = rf.at[g, mine + at_x(n_x - j)]
        return tx(("sf", g, j), ref, ref, sib)

    def t_y(g, j):
        return tx(("y", g, j), gt.at[g, at_y(j)], fy.at[g, j - 1], {"ray": at_y(j)})

    def t_z(g, j):
        return tx(("z", g, j), xb.at[g, y], xb.at[g, y], {"ray": at_y(j)})

    def t_w(g, j):
        return tx(("w", g, j), xf.at[g, y], xf.at[g, y], {"ray": at_y(j)})

    def t_qx(j):
        return tx(("qx", j), sqr.at[pix], sqr.at[pix], {"pix": lax.rem(pix + j, ring_x)})

    def t_qy(j):
        return tx(("qy", j), sqc.at[y], sqc.at[y], {"ray": at_y(j)})

    barrier = pltpu.get_barrier_semaphore()
    for j in range(1, ring_x):
        pl.semaphore_signal(barrier, inc=1, device_id={"pix": lax.rem(pix + j, ring_x)}, device_id_type=MESH)
    for j in others_y:
        pl.semaphore_signal(barrier, inc=1, device_id={"ray": at_y(j)}, device_id_type=MESH)

    def load_a(part, k):
        base = theirs if part == 0 else mine
        low = min(CHUNKS[k][1], own_rows - packed - CHUNKS[k][0])
        owners = pl.ds(base, n_x)
        return [pltpu.make_async_copy(a_hbm.at[owners, sl], a_v.at[owners, sl], a_sem.at[part, k, i])
                for i, sl in enumerate((rows(k), pl.ds(packed + CHUNKS[k][0], low)))]

    load_b = pltpu.make_async_copy(b_hbm.at[mine + x], b_v.at[pl.ds(0, own_rows)], b_sem)
    load_b.start()
    for k in chunks:
        for part in (0, 1):
            for t in load_a(part, k):
                t.start()
    pad = 2 * packed - own_rows
    a_v[:, pl.ds(own_rows, pad)] = jnp.zeros((ring_x, pad, width), BF16)
    b_v[pl.ds(own_rows, pad)] = jnp.zeros((pad, lanes), F32)
    sqv[...] = jnp.zeros_like(sqv)

    def first_half(shape):
        return lax.broadcasted_iota(jnp.int32, shape, len(shape) - 1) < half

    def swap(v):
        return pltpu.roll(v, half, 1)

    image = x_in[...]
    keep = first_half(image.shape)
    first = jnp.where(keep, image, 0.0)
    second = jnp.where(keep, 0.0, image)
    xn[0, 0] = first.astype(BF16)
    xn[0, 1] = swap(first).astype(BF16)
    xn[1, 0] = swap(second).astype(BF16)
    xn[1, 1] = second.astype(BF16)
    xf[...] = image.T.reshape(xf.shape)
    for g in range(GROUPS):
        xs[g] = xf[g, y]
    weights = rinv_in[pl.ds(mine + x, 1)]
    weights = jnp.broadcast_to(weights, (lanes, weights.shape[1])).T
    rinv[...] = jnp.where(first_half((packed, lanes)), weights[:packed], weights[packed:2 * packed])
    load_b.wait()
    top, low = b_v[pl.ds(0, packed)], b_v[pl.ds(packed, packed)]
    keep = first_half(top.shape)
    bp[0] = jnp.where(keep, top, swap(low))
    bp[1] = jnp.where(keep, swap(top), low)
    pl.semaphore_wait(barrier, ring_x - 1 + ring_y - 1)

    def block(part, k):
        base = theirs if part == 0 else mine
        n = CHUNKS[k][1]
        return (a_v[pl.ds(base, n_x), rows(k)].reshape(n_x * n, width),
                a_v[pl.ds(base, n_x), low_rows(k)].reshape(n_x * n, width))

    def F(g, s, part, k):
        if g == 0:
            @pl.when(s == 0)
            def _():
                for t in load_a(part, k):
                    t.wait()
        upper, lower = block(part, k)
        out = (jnp.dot(upper, xn[g, 0], preferred_element_type=F32)
               + jnp.dot(lower, xn[g, 1], preferred_element_type=F32))
        dst = ps if part == 0 else ss
        dst[g, :, rows(k)] = out.reshape(n_x, CHUNKS[k][1], lanes)
        if part == 0:
            t_p(g, k).start()

    def D(g, s, k):
        t_p(g, k).wait_recv()
        ss[g, :, rows(k)] = ss[g, :, rows(k)] + pd[g, :, rows(k)]
        for j in others_x:
            t_x(g, k, j).start()

    def O(g, s, k):
        for j in others_x:
            t_x(g, k, j).wait_recv()
        total = ss[g, x, rows(k)]
        for j in others_x:
            total = total + fin[g, j - 1, rows(k)]
        r = rinv[rows(k)] * (bp[g, rows(k)] - total)
        rall[g, mine + x, rows(k)] = r.astype(BF16)
        rf[g, mine + x, rows(k)] = r
        for j in others_x:
            t_r(g, k, j).start()
        t_s(g, k, 0).start()
        part = jnp.sum(r * r, axis=0, keepdims=True)
        sqv[g, pl.ds(s, 1)] = sqv[g, pl.ds(s, 1)] + part

    def A(g, s, k):
        for j in others_x:
            t_r(g, k, j).wait_recv()
            t_s(g, k, j).start()

    def B(g, s, part, k):
        if part == 0:
            for j in range(n_x):
                t_s(g, k, j).wait_recv()
        upper, lower = block(part, k)
        base = theirs if part == 0 else mine
        rt = rall[g, pl.ds(base, n_x), rows(k)].reshape(n_x * CHUNKS[k][1], lanes).T
        out = (jnp.dot(rt[:half], upper, preferred_element_type=F32)
               + jnp.dot(rt[half:], lower, preferred_element_type=F32)).reshape(n_y, cy, width)
        if part == 1 and k == 0:
            gt[g] = out
        else:
            gt[g] = gt[g] + out

    def Y0(g, s):
        for j in others_y:
            t_y(g, j).start()

        @pl.when(s == SWEEPS - 1)
        def _():
            for j in others_x:
                t_rf(g, j).start()
            t_sf(g, 0).start()

    def Y1(g, s):
        for j in others_y:
            t_y(g, j).wait_recv()
        total = gt[g, y]
        for j in others_y:
            total = total + fy[g, j - 1]
        image = xs[g] + lam[0] * cinv[...] * total
        xs[g] = image

        @pl.when(s < SWEEPS - 1)
        def _():
            xb[g, y] = image.astype(BF16)
            for j in others_y:
                t_z(g, j).start()

        @pl.when(s == SWEEPS - 1)
        def _():
            xf[g, y] = image
            for j in others_y:
                t_w(g, j).start()

    def Y2(g, s):
        @pl.when(s < SWEEPS - 1)
        def _():
            for j in others_y:
                t_z(g, j).wait_recv()
            image = xb[g].reshape(n_y * cy, width)
            none = jnp.zeros_like(image)
            xn[g, 0] = jnp.concatenate([image, none], axis=0).T
            xn[g, 1] = jnp.concatenate([none, image], axis=0).T
            for j in others_y:
                t_z(g, j).wait_send()

        @pl.when(s == SWEEPS - 1)
        def _():
            for j in others_x:
                t_rf(g, j).wait_recv()
                t_sf(g, j).start()
            for j in others_y:
                t_w(g, j).wait_recv()
                t_w(g, j).wait_send()

        for k in chunks:
            t_p(g, k).wait_send()
            for j in others_x:
                t_x(g, k, j).wait_send()
                t_r(g, k, j).wait_send()
            for j in range(n_x):
                t_s(g, k, j).wait_send()
        for j in others_y:
            t_y(g, j).wait_send()

    def Q0():
        sqr[pix] = sqv[...]
        for j in range(1, ring_x):
            t_qx(j).start()

    def Q1():
        for j in range(1, ring_x):
            t_qx(j).wait_recv()
        total = sqr[0]
        for j in range(1, ring_x):
            total = total + sqr[j]
        sqc[y] = total
        for j in others_y:
            t_qy(j).start()

    ORDER = (
        "aF00", "bA1", "aF10", "bB11", "bA2", "bB00", "aD0", "bB01",
        "aF01", "bB02", "bB12", "bY0", "aF11", "aD1", "aF02", "aF12",
        "aD2", "aO0", "bY1", "aO1", "aO2", "aA0", "aB10", "bY2",
    )
    TABLE = {"D": D, "O": O, "A": A}

    def run(op, g, s):
        if op[0] == "F":
            F(g, s, int(op[1]), int(op[2]))
        elif op[0] == "B":
            B(g, s, int(op[1]), int(op[2]))
        elif op[0] == "Y":
            (Y0, Y1, Y2)[int(op[1])](g, s)
        else:
            TABLE[op[0]](g, s, int(op[1]))

    def half_sweep(a, sa, b, sb, guard):
        for op in ORDER:
            g, s = (a, sa) if op[0] == "a" else (b, sb)
            if guard:
                pl.when(sa < SWEEPS if op[0] == "a" else sb >= 0)(functools.partial(run, op[1:], g, s))
                if op in ("bY0", "bY1"):
                    pl.when(sb == SWEEPS - 1)(Q0 if op == "bY0" else Q1)
            else:
                run(op[1:], g, s)

    def body(s, _):
        half_sweep(0, s, 1, s - 1, True)

        @pl.when(s < SWEEPS)
        def _():
            half_sweep(1, s, 0, s, False)
        return 0

    lax.fori_loop(0, SWEEPS + 1, body, 0)

    put_x = pltpu.make_async_copy(xf, x_out, x_sem)
    put_x.start()
    for g in range(GROUPS):
        for j in range(n_x):
            t_sf(g, j).wait_recv()
    put_r = pltpu.make_async_copy(rf, r_out, r_sem)
    put_r.start()
    for j in others_y:
        t_qy(j).wait_recv()
    total = sqc[0]
    for j in others_y:
        total = total + sqc[j]
    s_out[...] = total / ray_total
    put_x.wait()
    put_r.wait()
    for g in range(GROUPS):
        for j in others_x:
            t_rf(g, j).wait_send()
        for j in range(n_x):
            t_sf(g, j).wait_send()
    for j in range(1, ring_x):
        t_qx(j).wait_send()
    for j in others_y:
        t_qy(j).wait_send()


def _finish(rf, xf, sq, x_out, r_out, s_out):
    packed, lanes = rf.shape[2], rf.shape[3]
    left = lax.broadcasted_iota(jnp.int32, (packed, lanes), 1) < lanes // GROUPS

    def swap(v):
        return pltpu.roll(v, lanes // GROUPS, 1)

    for i in range(r_out.shape[0]):
        one, two = rf[0, i], rf[1, i]
        r_out[i, pl.ds(0, packed)] = jnp.where(left, one, swap(two))
        rest = r_out.shape[1] - packed
        r_out[i, pl.ds(packed, rest)] = jnp.where(left, swap(one), two)[:rest]

    @pl.when(pl.program_id(0) == 0)
    def _():
        x_out[...] = xf[...].reshape(lanes, x_out.shape[0]).T
        both = [sq[g] + swap(sq[g]) for g in range(GROUPS)]
        s_out[...] = jnp.where(left[:8], both[0], both[1])[:SWEEPS]


def solution(mesh):
    ring_x, ring_y = mesh.shape["pix"], mesh.shape["ray"]

    def local_sweeps(a_blk, x_loc, sino_loc, row_inv, col_inv, relaxation):
        rays, width = a_blk.shape
        cols = x_loc.shape[1]
        rp, cy, n_x = rays // ring_x, cols // ring_y // GROUPS, ring_x // 2
        packed = sum(n for _, n in CHUNKS)
        lane_rows = -(-2 * packed // 128) * 128
        rinv = jnp.pad(row_inv.reshape(ring_x, rp), ((0, 0), (0, lane_rows - rp)))
        cinv = col_inv.reshape(1, width)
        vmem = pl.BlockSpec(memory_space=pltpu.VMEM)
        hbm = pl.BlockSpec(memory_space=pl.ANY)
        smem = pl.BlockSpec(memory_space=pltpu.SMEM)
        x_part, r_part, s_part = pl.pallas_call(
            functools.partial(_kernel, ring_x, ring_y, rays * ring_y),
            out_shape=(
                jax.ShapeDtypeStruct((GROUPS, ring_y, cy, width), F32),
                jax.ShapeDtypeStruct((GROUPS, ring_x, packed, cols), F32),
                jax.ShapeDtypeStruct((GROUPS, 8, cols), F32),
            ),
            in_specs=[hbm, vmem, hbm, vmem, vmem, smem],
            out_specs=(hbm, hbm, vmem),
            scratch_shapes=[
                pltpu.VMEM((ring_x, 2 * packed, width), BF16),
                pltpu.VMEM((2 * packed, cols), F32),
                pltpu.VMEM((packed, cols), F32),
                pltpu.VMEM((GROUPS, packed, cols), F32),
                pltpu.VMEM((GROUPS, n_x, packed, cols), F32),
                pltpu.VMEM((GROUPS, n_x, packed, cols), F32),
                pltpu.VMEM((GROUPS, n_x, packed, cols), F32),
                pltpu.VMEM((GROUPS, n_x - 1, packed, cols), F32),
                pltpu.VMEM((GROUPS, ring_x, packed, cols), BF16),
                pltpu.VMEM((GROUPS, ring_x, packed, cols), F32),
                pltpu.VMEM((GROUPS, ring_y, cy, width), F32),
                pltpu.VMEM((GROUPS, ring_y - 1, cy, width), F32),
                pltpu.VMEM((GROUPS, cy, width), F32),
                pltpu.VMEM((GROUPS, ring_y, cy, width), BF16),
                pltpu.VMEM((GROUPS, ring_y, cy, width), F32),
                pltpu.VMEM((GROUPS, 2, width, cols), BF16),
                pltpu.VMEM((GROUPS, 8, cols), F32),
                pltpu.VMEM((ring_x, GROUPS, 8, cols), F32),
                pltpu.VMEM((ring_y, GROUPS, 8, cols), F32),
                pltpu.SemaphoreType.DMA((2, len(CHUNKS), 2)),
                pltpu.SemaphoreType.DMA,
                pltpu.SemaphoreType.DMA,
                pltpu.SemaphoreType.DMA,
                pltpu.SemaphoreType.DMA((160,)),
                pltpu.SemaphoreType.DMA((160,)),
            ],
            compiler_params=pltpu.CompilerParams(
                collective_id=0, has_side_effects=True, vmem_limit_bytes=60 * 1024 * 1024),
        )(a_blk.reshape(ring_x, rp, width), x_loc, sino_loc.reshape(ring_x, rp, cols), rinv, cinv, relaxation.reshape(1))
        step = ring_x // 4
        x_fin, resid, sq = pl.pallas_call(
            _finish,
            grid=(ring_x // step,),
            out_shape=(
                jax.ShapeDtypeStruct((width, cols), F32),
                jax.ShapeDtypeStruct((ring_x, rp, cols), F32),
                jax.ShapeDtypeStruct((SWEEPS, cols), F32),
            ),
            in_specs=[
                pl.BlockSpec((GROUPS, step, packed, cols), lambda i: (0, i, 0, 0)),
                pl.BlockSpec((GROUPS, ring_y, cy, width), lambda i: (0, 0, 0, 0)),
                pl.BlockSpec((GROUPS, 8, cols), lambda i: (0, 0, 0)),
            ],
            out_specs=(
                pl.BlockSpec((width, cols), lambda i: (0, 0)),
                pl.BlockSpec((step, rp, cols), lambda i: (i, 0, 0)),
                pl.BlockSpec((SWEEPS, cols), lambda i: (0, 0)),
            ),
        )(r_part, x_part, s_part)
        return x_fin, resid.reshape(rays, cols), sq

    return jax.shard_map(
        local_sweeps,
        mesh=mesh,
        in_specs=(P("ray", "pix"), P("pix", "part"), P("ray", "part"), P("ray"), P("pix"), P()),
        out_specs=(P("pix", "part"), P("ray", "part"), P(None, "part")),
        check_vma=False,
    )
```

time: 766 us -> 243 us (0.32); the launches traced: 757 us -> 243 us
  waiting for transfers between devices: 599 us -> 0 us
  Pallas kernels: 0 us -> 239 us
  matrix products: 115 us -> 0 us
  between operations: 15.4 us -> 1.29 us
  other arithmetic: 12.2 us -> 0 us
  blocking collectives: 8.83 us -> 0 us
    psum x12 -> x0, waiting for transfers between devices: 599 us -> none  [the longest x6 384 us: local_sweeps(): projected = lax.psum(part_proj, 'pix')]
    pallas_call x0 -> x2, Pallas kernels: none -> 239 us  [the longest x1 234 us: local_sweeps(): pl.pallas_call(functools.partial(_kernel, ring_x, ring_y, rays * ring_y),...]
    dot_general x12 -> x0, matrix products: 115 us -> none  [the longest x6 60.9 us: local_sweeps(): jnp.dot(a_blk, x_cur.astype(jnp.bfloat16), preferred_element_type=jnp.flo...]
    psum x1 -> x0, blocking collectives: 8.83 us -> none  [local_sweeps(): lax.psum(jnp.sum(residual * residual, axis=0), 'ray') / ray_total]
    reduce_sum x1 -> x0, other arithmetic: 8.03 us -> none  [local_sweeps(): jnp.sum(residual * residual, axis=0)]
  transfers between devices with their start and end apart: 12 -> 0, of which waited for: 12 -> 0; matrix products, arithmetic and copies ran while one was open for 0% -> 0% of each run, Pallas kernels for 0% -> 0%
where the time goes in v2:
time: 243 us
  Pallas kernels  239 us (98%)
  local copies, waits for them, and re-layouts  2.72 us (1%)
    pallas_call x1, Pallas kernels, local_sweeps(): pl.pallas_call(functools.partial(_kernel, ring_x, ring_y, rays * ring_y),...  234 us
    pallas_call x1, Pallas kernels, local_sweeps(): pl.pallas_call(_finish, grid=(ring_x // step,), out_shape=(jax.ShapeDtype...  5.17 us

profile of v2, /device:TPU:97, one launch (start us, length us, event | category | flops | bytes accessed | tf_op | source)
XLA Modules:
  0.0 242.8 jit_solution(17650941061974492845)
XLA Ops:
  1.3 1.3 reshape.27.cinv
  2.6 0.8 reshape.26
  3.4 0.6 pad.4.rinv_in
  4.0 233.6 %shard_map.85 = (f32[2,4,16,1152]{3,2,1,0:T(8,128)}, f32[2,8,368,128]{3,2,1,0:T(8,128)}, f32[2,8,128]{2,1,0:T(8,128)}) custom-call(bf16[8,720,1152]{2,1,0:T(8,128)(2,1)} %bitcast.5, f32[1152,128]{1,0:T(8,128)} %x_in.1, f32[8,720,128]{2,1,0:T(8,128)} %bitcast.6, f32[8,768]{1,0:T(8,128)} %pad.4.rinv_in, f32[1,1152]{1,0:T(1,128)} %reshape.27.cinv, f32[1]{0:T(128)} %bitcast.4.lam), custom_call_target="tpu_custom_call" | custom-call | tf_op jit(solution)/shard_map/pallas_call | solution.py:381
  237.6 5.2 %shard_map.86 = (f32[1152,128]{1,0:T(8,128)}, f32[8,720,128]{2,1,0:T(8,128)}, f32[6,128]{1,0:T(8,128)}) custom-call(f32[2,8,368,128]{3,2,1,0:T(8,128)} %get-tuple-element.9.rf, f32[2,4,16,1152]{3,2,1,0:T(8,128)} %get-tuple-element.10.xf, f32[2,8,128]{2,1,0:T(8,128)} %get-tuple-element.11.sq), custom_call_target="tpu_custom_call" | custom-call | tf_op jit(solution)/shard_map/pallas_call | solution.py:421

commit v3 on v2

--- a/solution.py
+++ b/solution.py
@@ -16,8 +16,8 @@
 CHUNKS = ((0, 128), (128, 128), (256, 112))
 
 
-def _kernel(ring_x, ring_y, ray_total, a_hbm, x_in, b_hbm, rinv_in, cinv, lam, x_out, r_out, s_out,
-            a_v, b_v, rinv, bp, ps, pd, ss, fin, rall, rf, gt, fy, xs, xb, xf, xn, sqv, sqr, sqc,
+def _kernel(ring_x, ring_y, ray_total, a_hbm, x_in, b_hbm, rinv_in, cinv_in, lam, x_out, r_out, s_out,
+            a_v, b_v, line, rinv, cinv, bp, ps, pd, ss, fin, rall, rf, gt, fy, xs, xb, xf, xn, sqv, sqr, sqc,
             a_sem, b_sem, x_sem, r_sem, send, recv):
     own_rows = b_hbm.shape[1]
     packed = ss.shape[2]
@@ -32,6 +32,11 @@
     mine, theirs = c * n_x, (1 - c) * n_x
     chunks = range(len(CHUNKS))
     others_x, others_y = range(1, n_x), range(1, n_y)
+    far_first_x = sorted(others_x, key=lambda j: -min(j, n_x - j))
+    far_first_y = sorted(others_y, key=lambda j: -min(j, n_y - j))
+    near_first_x = sorted(others_x, key=lambda j: min(j, n_x - j))
+    first_lanes = -(-width // 256) * 128
+    parts_y = (pl.ds(0, first_lanes), pl.ds(first_lanes, width - first_lanes))
 
     def at_x(j):
         return lax.rem(x + j, n_x)
@@ -78,14 +83,16 @@
         ref = rf.at[g, mine + at_x(n_x - j)]
         return tx(("sf", g, j), ref, ref, sib)
 
-    def t_y(g, j):
-        return tx(("y", g, j), gt.at[g, at_y(j)], fy.at[g, j - 1], {"ray": at_y(j)})
-
-    def t_z(g, j):
-        return tx(("z", g, j), xb.at[g, y], xb.at[g, y], {"ray": at_y(j)})
-
-    def t_w(g, j):
-        return tx(("w", g, j), xf.at[g, y], xf.at[g, y], {"ray": at_y(j)})
+    def t_y(g, i, j):
+        return tx(("y", g, i, j), gt.at[g, at_y(j), :, parts_y[i]], fy.at[g, j - 1, :, parts_y[i]], {"ray": at_y(j)})
+
+    def t_z(g, i, j):
+        ref = xb.at[g, y, :, parts_y[i]]
+        return tx(("z", g, i, j), ref, ref, {"ray": at_y(j)})
+
+    def t_w(g, i, j):
+        ref = xf.at[g, y, :, parts_y[i]]
+        return tx(("w", g, i, j), ref, ref, {"ray": at_y(j)})
 
     def t_qx(j):
         return tx(("qx", j), sqr.at[pix], sqr.at[pix], {"pix": lax.rem(pix + j, ring_x)})
@@ -134,9 +141,18 @@
     xf[...] = image.T.reshape(xf.shape)
     for g in range(GROUPS):
         xs[g] = xf[g, y]
-    weights = rinv_in[pl.ds(mine + x, 1)]
-    weights = jnp.broadcast_to(weights, (lanes, weights.shape[1])).T
-    rinv[...] = jnp.where(first_half((packed, lanes)), weights[:packed], weights[packed:2 * packed])
+    start = (mine + x) * own_rows
+    tile = rinv_in.shape[1]
+    for i in range(line.shape[1] // tile):
+        row = rinv_in[pl.ds(lax.rem(start // tile + i, rinv_in.shape[0]), 1)]
+        line[:, pl.ds(i * tile, tile)] = jnp.broadcast_to(row, (8, tile))
+    for i in range(cinv_in.shape[0]):
+        cinv[:, pl.ds(i * tile, tile)] = jnp.broadcast_to(cinv_in[pl.ds(i, 1)], (cy, tile))
+    weights = pltpu.roll(line[...], lax.rem(line.shape[1] - lax.rem(start, tile), line.shape[1]), 1)
+    weights = jnp.broadcast_to(weights[:1], (lanes, line.shape[1])).T
+    real = lax.broadcasted_iota(jnp.int32, (packed, lanes), 0) < own_rows - packed
+    rinv[...] = jnp.where(first_half((packed, lanes)), weights[:packed],
+                          jnp.where(real, weights[packed:2 * packed], 0.0))
     load_b.wait()
     top, low = b_v[pl.ds(0, packed)], b_v[pl.ds(packed, packed)]
     keep = first_half(top.shape)
@@ -167,7 +183,7 @@
     def D(g, s, k):
         t_p(g, k).wait_recv()
         ss[g, :, rows(k)] = ss[g, :, rows(k)] + pd[g, :, rows(k)]
-        for j in others_x:
+        for j in far_first_x:
             t_x(g, k, j).start()
 
     def O(g, s, k):
@@ -179,14 +195,14 @@
         r = rinv[rows(k)] * (bp[g, rows(k)] - total)
         rall[g, mine + x, rows(k)] = r.astype(BF16)
         rf[g, mine + x, rows(k)] = r
-        for j in others_x:
+        for j in far_first_x:
             t_r(g, k, j).start()
         t_s(g, k, 0).start()
         part = jnp.sum(r * r, axis=0, keepdims=True)
         sqv[g, pl.ds(s, 1)] = sqv[g, pl.ds(s, 1)] + part
 
     def A(g, s, k):
-        for j in others_x:
+        for j in near_first_x:
             t_r(g, k, j).wait_recv()
             t_s(g, k, j).start()
 
@@ -205,56 +221,68 @@
             gt[g] = gt[g] + out
 
     def Y0(g, s):
-        for j in others_y:
-            t_y(g, j).start()
+        for i in (0, 1):
+            for j in far_first_y:
+                t_y(g, i, j).start()
 
         @pl.when(s == SWEEPS - 1)
         def _():
-            for j in others_x:
+            for j in far_first_x:
                 t_rf(g, j).start()
             t_sf(g, 0).start()
 
+    def update(g, s, i):
+        for j in others_y:
+            t_y(g, i, j).wait_recv()
+        lanes_i = parts_y[i]
+        total = gt[g, y, :, lanes_i]
+        for j in others_y:
+            total = total + fy[g, j - 1, :, lanes_i]
+        image = xs[g, :, lanes_i] + lam[0] * cinv[:, lanes_i] * total
+        xs[g, :, lanes_i] = image
+
+        @pl.when(s < SWEEPS - 1)
+        def _():
+            xb[g, y, :, lanes_i] = image.astype(BF16)
+            for j in far_first_y:
+                t_z(g, i, j).start()
+
+        @pl.when(s == SWEEPS - 1)
+        def _():
+            xf[g, y, :, lanes_i] = image
+            for j in far_first_y:
+                t_w(g, i, j).start()
+
     def Y1(g, s):
-        for j in others_y:
-            t_y(g, j).wait_recv()
-        total = gt[g, y]
-        for j in others_y:
-            total = total + fy[g, j - 1]
-        image = xs[g] + lam[0] * cinv[...] * total
-        xs[g] = image
-
-        @pl.when(s < SWEEPS - 1)
-        def _():
-            xb[g, y] = image.astype(BF16)
-            for j in others_y:
-                t_z(g, j).start()
-
-        @pl.when(s == SWEEPS - 1)
-        def _():
-            xf[g, y] = image
-            for j in others_y:
-                t_w(g, j).start()
+        update(g, s, 0)
+
+    def Y3(g, s):
+        update(g, s, 1)
 
     def Y2(g, s):
         @pl.when(s < SWEEPS - 1)
         def _():
-            for j in others_y:
-                t_z(g, j).wait_recv()
+            for i in (0, 1):
+                for j in others_y:
+                    t_z(g, i, j).wait_recv()
             image = xb[g].reshape(n_y * cy, width)
-            none = jnp.zeros_like(image)
-            xn[g, 0] = jnp.concatenate([image, none], axis=0).T
-            xn[g, 1] = jnp.concatenate([none, image], axis=0).T
-            for j in others_y:
-                t_z(g, j).wait_send()
+            both = jnp.concatenate([image, image], axis=0).T
+            keep = first_half(both.shape)
+            xn[g, 0] = jnp.where(keep, both, jnp.zeros_like(both))
+            xn[g, 1] = jnp.where(keep, jnp.zeros_like(both), both)
+            for i in (0, 1):
+                for j in others_y:
+                    t_z(g, i, j).wait_send()
 
         @pl.when(s == SWEEPS - 1)
         def _():
-            for j in others_x:
+            for j in near_first_x:
                 t_rf(g, j).wait_recv()
                 t_sf(g, j).start()
-            for j in others_y:
-                t_w(g, j).wait_recv()
-                t_w(g, j).wait_send()
+            for i in (0, 1):
+                for j in others_y:
+                    t_w(g, i, j).wait_recv()
+                    t_w(g, i, j).wait_send()
 
         for k in chunks:
             t_p(g, k).wait_send()
@@ -263,8 +291,9 @@
                 t_r(g, k, j).wait_send()
             for j in range(n_x):
                 t_s(g, k, j).wait_send()
-        for j in others_y:
-            t_y(g, j).wait_send()
+        for i in (0, 1):
+            for j in others_y:
+                t_y(g, i, j).wait_send()
 
     def Q0():
         sqr[pix] = sqv[...]
@@ -282,9 +311,10 @@
             t_qy(j).start()
 
     ORDER = (
-        "aF00", "bA1", "aF10", "bB11", "bA2", "bB00", "aD0", "bB01",
-        "aF01", "bB02", "bB12", "bY0", "aF11", "aD1", "aF02", "aF12",
-        "aD2", "aO0", "bY1", "aO1", "aO2", "aA0", "aB10", "bY2",
+        "aF02", "bA0", "aF00", "bA2", "aF10", "bB10", "bB12", "aD0",
+        "bA1", "bB00", "bB11", "bB02", "bB01", "bY0", "aF12", "aD2",
+        "aF01", "aF11", "aD1", "aO0", "bY1", "bY3", "aO2", "aO1",
+        "bY2",
     )
     TABLE = {"D": D, "O": O, "A": A}
 
@@ -294,7 +324,7 @@
         elif op[0] == "B":
             B(g, s, int(op[1]), int(op[2]))
         elif op[0] == "Y":
-            (Y0, Y1, Y2)[int(op[1])](g, s)
+            (Y0, Y1, Y2, Y3)[int(op[1])](g, s)
         else:
             TABLE[op[0]](g, s, int(op[1]))
 
@@ -357,7 +387,7 @@
         rest = r_out.shape[1] - packed
         r_out[i, pl.ds(packed, rest)] = jnp.where(left, swap(one), two)[:rest]
 
-    @pl.when(pl.program_id(0) == 0)
+    @pl.when(pl.program_id(0) == 1)
     def _():
         x_out[...] = xf[...].reshape(lanes, x_out.shape[0]).T
         both = [sq[g] + swap(sq[g]) for g in range(GROUPS)]
@@ -372,9 +402,8 @@
         cols = x_loc.shape[1]
         rp, cy, n_x = rays // ring_x, cols // ring_y // GROUPS, ring_x // 2
         packed = sum(n for _, n in CHUNKS)
-        lane_rows = -(-2 * packed // 128) * 128
-        rinv = jnp.pad(row_inv.reshape(ring_x, rp), ((0, 0), (0, lane_rows - rp)))
-        cinv = col_inv.reshape(1, width)
+        rinv = row_inv.reshape(-1, 128)
+        cinv = col_inv.reshape(-1, 128)
         vmem = pl.BlockSpec(memory_space=pltpu.VMEM)
         hbm = pl.BlockSpec(memory_space=pl.ANY)
         smem = pl.BlockSpec(memory_space=pltpu.SMEM)
@@ -390,7 +419,9 @@
             scratch_shapes=[
                 pltpu.VMEM((ring_x, 2 * packed, width), BF16),
                 pltpu.VMEM((2 * packed, cols), F32),
+                pltpu.VMEM((8, (-(-rp // 128) + 1) * 128), F32),
                 pltpu.VMEM((packed, cols), F32),
+                pltpu.VMEM((cy, width), F32),
                 pltpu.VMEM((GROUPS, packed, cols), F32),
                 pltpu.VMEM((GROUPS, n_x, packed, cols), F32),
                 pltpu.VMEM((GROUPS, n_x, packed, cols), F32),
@@ -411,13 +442,13 @@
                 pltpu.SemaphoreType.DMA,
                 pltpu.SemaphoreType.DMA,
                 pltpu.SemaphoreType.DMA,
-                pltpu.SemaphoreType.DMA((160,)),
-                pltpu.SemaphoreType.DMA((160,)),
+                pltpu.SemaphoreType.DMA((192,)),
+                pltpu.SemaphoreType.DMA((192,)),
             ],
             compiler_params=pltpu.CompilerParams(
                 collective_id=0, has_side_effects=True, vmem_limit_bytes=60 * 1024 * 1024),
         )(a_blk.reshape(ring_x, rp, width), x_loc, sino_loc.reshape(ring_x, rp, cols), rinv, cinv, relaxation.reshape(1))
-        step = ring_x // 4
+        step = ring_x // 2
         x_fin, resid, sq = pl.pallas_call(
             _finish,
             grid=(ring_x // step,),

time: 243 us -> 231 us (0.951)
  Pallas kernels: 239 us -> 230 us
  local copies, waits for them, and re-layouts: 2.72 us -> 0 us
    pallas_call x1, Pallas kernels: 234 us -> 226 us  [local_sweeps(): pl.pallas_call(functools.partial(_kernel, ring_x, ring_y, rays * ring_y),...]
where the time goes in v3:
time: 231 us
  Pallas kernels  230 us (100%)
    pallas_call x1, Pallas kernels, local_sweeps(): pl.pallas_call(functools.partial(_kernel, ring_x, ring_y, rays * ring_y),...  226 us

profile of v3, /device:TPU:97, one launch (start us, length us, event | category | flops | bytes accessed | tf_op | source)
XLA Modules:
  0.0 231.2 jit_solution(12827271902720463524)
XLA Ops:
  1.3 225.9 %shard_map.85 = (f32[2,4,16,1152]{3,2,1,0:T(8,128)}, f32[2,8,368,128]{3,2,1,0:T(8,128)}, f32[2,8,128]{2,1,0:T(8,128)}) custom-call(bf16[8,720,1152]{2,1,0:T(8,128)(2,1)} %bitcast.7, f32[1152,128]{1,0:T(8,128)} %x_in.1, f32[8,720,128]{2,1,0:T(8,128)} %bitcast.8, f32[45,128]{1,0:T(8,128)} %bitcast.9, f32[9,128]{1,0:T(8,128)} %bitcast.10, f32[1]{0:T(128)} %bitcast.6.lam), custom_call_target="tpu_custom_call" | custom-call | tf_op jit(solution)/shard_map/pallas_call | solution.py:410
  227.2 4.0 %shard_map.86 = (f32[1152,128]{1,0:T(8,128)}, f32[8,720,128]{2,1,0:T(8,128)}, f32[6,128]{1,0:T(8,128)}) custom-call(f32[2,8,368,128]{3,2,1,0:T(8,128)} %get-tuple-element.9.rf, f32[2,4,16,1152]{3,2,1,0:T(8,128)} %get-tuple-element.10.xf, f32[2,8,128]{2,1,0:T(8,128)} %get-tuple-element.11.sq), custom_call_target="tpu_custom_call" | custom-call | tf_op jit(solution)/shard_map/pallas_call | solution.py:452
